TPU v7x, 32 devices: a whole 2x2x4 slice. The times are simulated.
32 devices in a mesh: seq: 4 (over y, x), rep: 8 (over z, core).
Axes of the slice: x: 2, y: 2, z: 4, core: 2. Of those that a mesh axis runs over, the one named last changes fastest.
Arguments:
- tile_embed: bfloat16 [8, 4096, 768], P('rep', 'seq'), may hold values from -6 to 6
- tile_source: int32 [8, 4096], P('rep', 'seq'), may hold values from 0 to 4095, as said below
- slide_len: int32 [8], P('rep'), may hold values from 2048 to 4096
- grad_out: bfloat16 [8, 4096, 768], P('rep', 'seq'), may hold values from -6 to 6
- w_query: bfloat16 [768, 768], replicated, may hold values from -0.11727427342914273 to 0.11727427342914273
- w_key: bfloat16 [768, 768], replicated, may hold values from -0.11727427342914273 to 0.11727427342914273
- w_value: bfloat16 [768, 768], replicated, may hold values from -0.21875 to 0.21875
- w_out: bfloat16 [768, 768], replicated, may hold values from -0.21875 to 0.21875
Outputs:
- encoded: bfloat16 [8, 4096, 768], P('rep', 'seq')
- embed_grad: bfloat16 [8, 4096, 768], P('rep', 'seq')
- grad_query: float32 [768, 768], replicated
- grad_key: float32 [768, 768], replicated
- grad_value: float32 [768, 768], replicated
- grad_outproj: float32 [768, 768], replicated
Inputs may be any that keep to these rules, and one draw needn't show every extreme that they name: For each slide, tile_source is a permutation of 0 to 4095; each run of 1024 slide positions (aligned) takes exactly 1024 // (number of such runs) rows from each aligned run of 1024 rows of tile_embed.
All inputs are finite; a program needn't handle non-finite values.
Results may differ from a plain program's by a relative error of at most 0.0025.
The roundings to bfloat16 on the way count: a program that leaves them out, or rounds other values in their place, can miss the bound.
Values may be sent and summed in bfloat16 or wider, within the bound.
No kernel may reach another device: no remote copies, remote signals or barrier semaphores. Data moves between devices by JAX's collectives and lax.ppermute only.
A program may use at most 192 MiB of HBM per device.

v0:
```python
import jax
import jax.numpy as jnp
from jax import lax
from jax.sharding import PartitionSpec as P

HEADS = 16
SEG = 1024
RATE = 16
NEGATIVE = -1e30


def chosen(dilation, head_count):
    return jnp.arange(dilation)[:, None] == (jnp.arange(head_count) % dilation)[None, :]


def sparse_rows(dense, dilation):
    row_count, head_count, trailing = dense.shape
    blocks = dense.astype(jnp.float32).reshape(
        row_count // dilation, dilation, head_count, trailing
    )
    selected = chosen(dilation, head_count)[None, :, :, None]
    return jnp.sum(jnp.where(selected, blocks, jnp.float32(0.0)), axis=1)


def spread_rows(sparse, dilation, filler):
    row_count, head_count, trailing = sparse.shape
    selected = chosen(dilation, head_count)[None, :, :, None]
    spread = jnp.where(selected, sparse[:, None], jnp.float32(filler))
    return spread.reshape(row_count * dilation, head_count, trailing)


def product(pattern, left_side, right_side):
    return jnp.einsum(pattern, left_side, right_side, preferred_element_type=jnp.float32)


def masked_scores(queries, key_rows, key_ok, pieces, scaling):
    scores = product("nqd,nkd->nqk", queries, key_rows) * scaling
    return jnp.where(key_ok.reshape(pieces, 1, -1), scores, NEGATIVE)


def head_forward(queries, key_rows, values, key_ok, pieces, scaling):
    head_width = queries.shape[-1]
    queries = queries.reshape(pieces, -1, head_width)
    key_rows = key_rows.reshape(pieces, -1, head_width)
    values = values.reshape(pieces, -1, head_width)
    scores = masked_scores(queries, key_rows, key_ok, pieces, scaling)
    maxima = jnp.max(scores, axis=-1)
    weights = jnp.exp(scores - maxima[..., None])
    totals = jnp.sum(weights, axis=-1)
    numerator = product("nqk,nkd->nqd", weights.astype(jnp.bfloat16), values)
    return (numerator.reshape(-1, head_width), maxima.reshape(-1), totals.reshape(-1))


def split_pieces(arrays, pieces):
    return tuple((member.reshape(pieces, -1, member.shape[-1]) for member in arrays))


def score_terms(queries, key_rows, values, key_ok, log_total, upstream, deltas, pieces, scaling):
    scores = masked_scores(queries, key_rows, key_ok, pieces, scaling)
    probabilities = jnp.exp(scores - log_total.reshape(pieces, -1, 1))
    prob_grad = product("nqd,nkd->nqk", upstream, values)
    score_grad = (probabilities * (prob_grad - deltas.reshape(pieces, -1, 1))).astype(jnp.bfloat16)
    return (probabilities, score_grad)


def head_backward(queries, key_rows, values, key_ok, log_total, upstream, deltas, pieces, scaling):
    head_width = queries.shape[-1]
    queries, key_rows, values, upstream = split_pieces(
        (queries, key_rows, values, upstream), pieces
    )
    probabilities, score_grad = score_terms(
        queries, key_rows, values, key_ok, log_total, upstream, deltas, pieces, scaling
    )
    value_grad = product("nqk,nqd->nkd", probabilities.astype(jnp.bfloat16), upstream)
    query_grad = product("nqk,nkd->nqd", score_grad, key_rows) * scaling
    key_grad = product("nqk,nqd->nkd", score_grad, queries) * scaling
    return (
        query_grad.reshape(-1, head_width),
        key_grad.reshape(-1, head_width),
        value_grad.reshape(-1, head_width),
    )


def heads_map(function, arrays, pieces, scaling):
    transposed = tuple((jnp.moveaxis(member, 1, 0) for member in arrays))
    results = lax.map(lambda members: function(*members, pieces, scaling), transposed)
    return tuple((jnp.moveaxis(member, 0, 1) for member in results))


def merge_parts(local_part, remote, dilation):
    numer_local, max_local, total_local = local_part
    numer_far = spread_rows(remote[0], dilation, 0.0)
    max_far = spread_rows(remote[1][..., None], dilation, NEGATIVE)[..., 0]
    total_far = spread_rows(remote[2][..., None], dilation, 0.0)[..., 0]
    highest = jnp.maximum(max_local, max_far)
    weight_local = jnp.exp(max_local - highest)
    weight_far = jnp.exp(max_far - highest)
    combined = total_local * weight_local + total_far * weight_far
    output = (numer_local * weight_local[..., None] + numer_far * weight_far[..., None]) / combined[
        ..., None
    ]
    return (output, highest + jnp.log(combined))


def project(left_side, right_side):
    return jnp.dot(left_side, right_side, preferred_element_type=jnp.float32)


def per_device(tile_embed, tile_source, slide_len, grad_out, w_query, w_key, w_value, w_out):
    owned_rows = tile_embed[0]
    source = tile_source[0]
    row_count, features = owned_rows.shape
    stripes = lax.axis_size("seq")
    stripe = lax.axis_index("seq")
    portion = row_count // stripes
    owner_dev = source // row_count
    ordering = jnp.argsort(owner_dev, stable=True)
    wanted = (source % row_count)[ordering].reshape(stripes, portion)
    requested = lax.all_to_all(wanted, "seq", split_axis=0, concat_axis=0, tiled=True)
    picked = jnp.take(owned_rows, requested.reshape(-1), axis=0).reshape(stripes, portion, features)
    arrived = lax.all_to_all(picked, "seq", split_axis=0, concat_axis=0, tiled=True).reshape(
        row_count, features
    )
    embedded = jnp.zeros_like(arrived).at[ordering].set(arrived)
    length = slide_len[0]
    upstream_in = grad_out[0]
    head_dim = features // HEADS
    scaling = head_dim ** (-0.5)
    positions = stripe * row_count + jnp.arange(row_count)
    valid_rows = positions < length
    queries = project(embedded, w_query).astype(jnp.bfloat16).reshape(row_count, HEADS, head_dim)
    key_rows = project(embedded, w_key).astype(jnp.bfloat16).reshape(row_count, HEADS, head_dim)
    values = project(embedded, w_value).astype(jnp.bfloat16).reshape(row_count, HEADS, head_dim)
    local_ok = jnp.broadcast_to(valid_rows[:, None], (row_count, HEADS))
    local_part = heads_map(
        head_forward, (queries, key_rows, values, local_ok), row_count // SEG, scaling
    )
    sparse_q = sparse_rows(queries, RATE).astype(jnp.bfloat16)
    sparse_k = sparse_rows(key_rows, RATE).astype(jnp.bfloat16)
    sparse_v = sparse_rows(values, RATE).astype(jnp.bfloat16)
    near_count = sparse_k.shape[0]
    far_k, far_v = (
        lax.all_gather(sparse_k.reshape(near_count, features), "seq", axis=0, tiled=True),
        lax.all_gather(sparse_v.reshape(near_count, features), "seq", axis=0, tiled=True),
    )
    far_count = far_k.shape[0]
    far_k = far_k.reshape(far_count, HEADS, head_dim)
    far_v = far_v.reshape(far_count, HEADS, head_dim)
    sparse_pos = jnp.arange(far_count)[:, None] * RATE + (jnp.arange(HEADS) % RATE)[None, :]
    sparse_ok = sparse_pos < length
    remote = heads_map(head_forward, (sparse_q, far_k, far_v, sparse_ok), 1, scaling)
    output, log_total = merge_parts(local_part, remote, RATE)
    attended = (
        (output * valid_rows[:, None, None]).astype(jnp.bfloat16).reshape(row_count, features)
    )
    encoded = (embedded.astype(jnp.float32) + project(attended, w_out)).astype(jnp.bfloat16)
    upstream = (
        (project(upstream_in, w_out.T) * valid_rows[:, None])
        .astype(jnp.bfloat16)
        .reshape(row_count, HEADS, head_dim)
    )
    deltas = jnp.sum(upstream.astype(jnp.float32) * output, axis=-1)
    grad_outproj = jnp.einsum(
        "td,te->de", attended, upstream_in, preferred_element_type=jnp.float32
    )
    local_grads = heads_map(
        head_backward,
        (queries, key_rows, values, local_ok, log_total, upstream, deltas),
        row_count // SEG,
        scaling,
    )
    sparse_up = sparse_rows(upstream, RATE).astype(jnp.bfloat16)
    sparse_delta = sparse_rows(deltas[..., None], RATE)[..., 0]
    sparse_total = sparse_rows(log_total[..., None], RATE)[..., 0]
    remote_grads = heads_map(
        head_backward,
        (sparse_q, far_k, far_v, sparse_ok, sparse_total, sparse_up, sparse_delta),
        1,
        scaling,
    )
    key_back, value_back = (
        lax.psum_scatter(
            remote_grads[1].reshape(far_count, features), "seq", scatter_dimension=0, tiled=True
        ),
        lax.psum_scatter(
            remote_grads[2].reshape(far_count, features), "seq", scatter_dimension=0, tiled=True
        ),
    )
    key_back = key_back.reshape(near_count, HEADS, head_dim)
    value_back = value_back.reshape(near_count, HEADS, head_dim)
    query_far = remote_grads[0]
    query_grad = (
        (local_grads[0] + spread_rows(query_far, RATE, 0.0))
        .astype(jnp.bfloat16)
        .reshape(row_count, features)
    )
    key_grad = (
        (local_grads[1] + spread_rows(key_back, RATE, 0.0))
        .astype(jnp.bfloat16)
        .reshape(row_count, features)
    )
    value_grad = (
        (local_grads[2] + spread_rows(value_back, RATE, 0.0))
        .astype(jnp.bfloat16)
        .reshape(row_count, features)
    )
    embed_grad = upstream_in.astype(jnp.float32) + project(query_grad, w_query.T)
    embed_grad = embed_grad + project(key_grad, w_key.T)
    embed_grad = (embed_grad + project(value_grad, w_value.T)).astype(jnp.bfloat16)
    grad_query = jnp.einsum("td,te->de", embedded, query_grad, preferred_element_type=jnp.float32)
    grad_key = jnp.einsum("td,te->de", embedded, key_grad, preferred_element_type=jnp.float32)
    grad_value = jnp.einsum("td,te->de", embedded, value_grad, preferred_element_type=jnp.float32)
    summed = lax.psum((grad_query, grad_key, grad_value, grad_outproj), ("seq", "rep"))
    return (encoded[None], embed_grad[None], summed[0], summed[1], summed[2], summed[3])


def solution(mesh):
    return jax.shard_map(
        per_device,
        mesh=mesh,
        in_specs=(
            P("rep", "seq", None),
            P("rep", "seq"),
            P("rep"),
            P("rep", "seq", None),
            P(),
            P(),
            P(),
            P(),
        ),
        out_specs=(P("rep", "seq", None), P("rep", "seq", None), P(), P(), P(), P()),
        check_vma=False,
    )
```

profile of v0, /device:TPU:0, one launch (start us, length us, event | category | flops | bytes accessed | tf_op | source)
XLA Modules:
  0.0 939.3 jit_solution(3229480369411910893)
XLA Ops:
  8.0 4.4 sort.17
  12.4 4.5 gather_fusion
  16.9 9.7 %all_to_all.14 = s32[4,1,256]{2,1,0:T(1,128)S(1)} all-to-all(s32[4,1,256]{2,1,0:T(1,128)S(1)} %bitcast.389), channel_id=1, replica_groups=mesh['seq'=4,'rep'=8] {'seq'}, dimensions={0} | all-to-all | bytes 8192 | tf_op jit(solution)/shard_map/all_to_all | solution.py:119
  26.6 4.0 gather_fusion.1
  32.0 4.5 all-to-all-start.1
  43.2 7.8 reshape.434
  53.0 4.9 copy.100
  58.0 6.4 scatter_custom_fusion
  69.7 7.8 reshape.431
  82.9 7.8 reshape.432
  90.7 4.3 convolution_convert_fusion
  98.1 7.8 reshape.433
  105.9 14.5 %select_reduce_fusion = (bf16[64,16,48]{2,1,0:T(8,128)(2,1)}, bf16[64,16,48]{2,1,0:T(8,128)(2,1)S(1)}, bf16[64,16,48]{2,1,0:T(8,128)(2,1)S(1)}, bf16[64,16,48]{2,1,0:T(8,128)(2,1)}) fusion(f32[64,16,16,48]{3,2,1,0:T(8,128)} %reshape.434, pred[16,16]{1,0:T(8,128)(4,1)S(1)} %iota_compare_fusion, f32[64,16,16,48]{3,2,1,0:T(8,128)} %reshape.432, ...), kind=kLoop, calls=%fused_computation.133 | loop fusion | flops 6094848 | bytes 12976384 | tf_op jit(solution)/shard_map/reduce_sum | solution.py:22
  120.6 10.6 %all_gather.6 = bf16[256,768]{1,0:T(8,128)(2,1)S(1)} all-gather(bf16[64,768]{1,0:T(8,128)(2,1)S(1)} %convert_element_type.144), channel_id=1, replica_groups=mesh['seq'=4,'rep'=8] {'seq'}, dimensions={0}, use_global_device_ids=true | all-gather | bytes 491520 | tf_op jit(solution)/shard_map/all_gather | solution.py:143
  132.2 8.9 all_gather.7
  143.7 26.0 %while.57 = (s32[]{:T(128)}, f32[16,64,48]{1,2,0:T(8,128)S(1)}, f32[16,64]{1,0:T(8,128)S(1)}, f32[16,64]{1,0:T(8,128)S(1)}, pred[16,256]{1,0:T(8,128)(4,1)S(1)},...) while((s32[]{:T(128)}, f32[16,64,48]{1,2,0:T(8,128)S(1)}, ...), condition=%wide.region_12.13_spmd, body=%wide.region_9.12_spmd.sunk | while | flops 3260290 | bytes 374129 | solution.py:86
  187.5 142.6 %while.56 = (s32[]{:T(128)}, f32[16,1024,48]{1,2,0:T(8,128)}, f32[16,1024]{1,0:T(8,128)S(1)}, f32[16,1024]{1,0:T(8,128)S(1)}, pred[16,1024]{1,0:T(8,128)(4,1)S(1...) while((s32[]{:T(128)}, f32[16,1024,48]{1,2,0:T(8,128)}, ...), condition=%wide.region_5.6_spmd, body=%wide.region_2.5_spmd.sunk | while | flops 212858880 | bytes 30383244 | solution.py:86
  210.1 4.0 fusion.202
  219.0 4.0 fusion.202
  228.0 4.0 fusion.202
  236.9 4.0 fusion.202
  245.8 4.0 fusion.202
  254.7 4.0 fusion.202
  263.6 4.0 fusion.202
  272.5 4.0 fusion.202
  281.5 4.0 fusion.202
  299.3 4.0 fusion.202
  308.2 4.0 fusion.202
  317.1 4.0 fusion.202
  326.0 4.0 fusion.202
  332.5 7.9 copy.83
  340.4 13.4 %multiply_convert_fusion.1 = (bf16[1024,16,48]{2,1,0:T(8,128)(2,1)}, f32[1024,16,48]{2,1,0:T(8,128)S(1)}) fusion(f32[1024]{0:T(1024)S(1)} %copy-done.34, f32[1024,16]{1,0:T(8,128)} %copy.97, f32[1024,16]{1,0:T(8,128)S(1)} %copy.96, f32[64,16,48]{2,1,0:T(8,128)S(1)} %copy.95, pred[1024,16]{1,0:T(8,128)(4,1)S(1)} %copy-done.19, f32[1024,16]{1,0:T(8,128)S(1)} %copy.93, ...), kind=kLoop, calls=%fused_computation.135 | loop fusion | flops 5505024 | bytes 8278016 | tf_op jit(solution)/shard_map/convert_element_type | solution.py:154
  357.3 98.4 %while.59 = (s32[]{:T(128)}, f32[16,64,48]{1,2,0:T(8,128)S(1)}, f32[16,256,48]{1,2,0:T(8,128)}, f32[16,256,48]{1,2,0:T(8,128)}, pred[16,256]{1,0:T(8,128)(4,1)},...) while((s32[]{:T(128)}, f32[16,64,48]{1,2,0:T(8,128)S(1)}, ...), condition=%wide.region_20.21_spmd, body=%wide.region_19.20_spmd.sunk | while | flops 7994370 | bytes 687741 | solution.py:86
  470.3 181.2 %while.58 = (s32[]{:T(128)}, f32[16,1024,48]{1,2,0:T(8,128)}, f32[16,1024,48]{1,2,0:T(8,128)}, f32[16,1024,48]{1,2,0:T(8,128)}, pred[16,1024]{1,0:T(8,128)(4,1)S...) while((s32[]{:T(128)}, f32[16,1024,48]{1,2,0:T(8,128)}, ...), condition=%wide.region_15.16_spmd, body=%wide.region_14.15_spmd.sunk | while | flops 513900544 | bytes 21337212 | solution.py:86
  651.8 7.9 copy.102
  659.6 7.8 copy.112
  667.5 7.9 copy.115
  675.3 5.5 copy.98
  680.8 4.2 fusion.114
  687.8 15.2 %fusion.110 = (bf16[1024,16,48]{2,1,0:T(8,128)(2,1)}, bf16[1024,16,48]{2,1,0:T(8,128)(2,1)}, bf16[1024,16,48]{2,1,0:T(8,128)(2,1)}) fusion(f32[16,1024,48]{2,0,1:T(8,128)} %copy.102, f32[64,16,48]{2,1,0:T(8,128)S(1)} %copy.110, pred[1024,16]{1,0:T(8,128)(4,1)} %copy.94, f32[64,16,48]{2,1,0:T(8,128)S(1)} %copy.113, f32[16,1024,48]{2,0,1:T(8,128)} %copy.112, ...), kind=kLoop, calls=%fused_computation.127 | loop fusion | flops 7077888 | bytes 14761984 | tf_op jit(solution)/shard_map/convert_element_type | solution.py:194
  703.0 5.5 copy.111
  708.5 4.2 fusion.130
  712.7 5.5 copy.114
  718.2 4.2 fusion.131
  722.5 4.4 copy.117
  727.0 4.2 fusion.132
  731.2 5.0 fusion.117
  742.9 179.8 %all-reduce.3.cloned.1.call-done = (f32[768,768]{1,0:T(8,128)}, f32[768,768]{1,0:T(8,128)}, f32[768,768]{1,0:T(8,128)}, f32[768,768]{1,0:T(8,128)}) async-done(((f32[768,768]{1,0:T(8,128)}, f32[768,768]{1,0:T(8,128)}, f32[768,768]{1,0:T(8,128)}, f32[768,768]{1,0:T(8,128)}), (f32[768,768]{1,0:T(8,128)}, f32[768,768]{1,0:T(8,128)}, f32[768,768]{1,0:T(8,128)}, ...) | async-done | bytes 9437200 | tf_op jit(solution)/shard_map/psum | solution.py:213
  (596 shorter events, 478.9 us)
Async XLA Ops:
  7.2 19.4 %copy-start = (bf16[1,1024,768]{2,1,0:T(8,128)(2,1)S(1)}, bf16[1,1024,768]{2,1,0:T(8,128)(2,1)}, u32[]{:S(2)}) copy-start(bf16[1,1024,768]{2,1,0:T(8,128)(2,1)} %param.16) | copy-start | bytes 4718596
  32.0 6.3 copy-start.13
  32.0 26.0 %all-to-all-start.1 = ((bf16[4,256,768]{2,1,0:T(8,128)(2,1)}), bf16[4,256,768]{2,1,0:T(8,128)(2,1)}, u32[]{:S(2)}, u32[]{:S(2)}) async-start(bf16[4,256,768]{2,1,0:T(8,128)(2,1)} %broadcast_select_fusion), calls=%async_computation.1 | async-start | bytes 3145728 | tf_op jit(solution)/shard_map/all_to_all | solution.py:121
  36.5 648.5 %reduce-scatter.7.cloned.1.call-start = ((), (), s32[]{:S(2)}) async-start(), calls=%async_computation.4 | async-start | bytes 983040
  41.0 12.0 %copy-start.4 = (bf16[1024,768]{0,1:T(8,128)(2,1)}, bf16[1024,768]{0,1:T(8,128)(2,1)S(1)}, u32[]{:S(2)}) copy-start(bf16[1024,768]{0,1:T(8,128)(2,1)S(1)} %multiply_convert_fusion.2) | copy-start | bytes 4718596
  52.1 5.8 copy-start.26
  64.4 3.3 copy-start.15
  80.7 10.1 %copy-start.6 = (bf16[1024,768]{0,1:T(8,128)(2,1)}, bf16[1024,768]{0,1:T(8,128)(2,1)S(1)}, u32[]{:S(2)}) copy-start(bf16[1024,768]{0,1:T(8,128)(2,1)S(1)} %convolution_convert_fusion.1) | copy-start | bytes 4718596
  131.2 12.4 %copy-start.35 = (f32[16,64]{1,0:T(8,128)S(1)}, f32[16,64]{1,0:T(8,128)}, u32[]{:S(2)}) copy-start(f32[16,64]{1,0:T(8,128)} %custom-call.7) | copy-start | bytes 12292
  169.6 3.2 copy-start.9
  169.6 3.2 copy-start.22
  169.7 9.4 copy-start.30
  173.8 5.2 copy-start.7
  179.0 3.2 copy-start.8
  182.2 3.2 copy-start.36
  182.2 5.2 copy-start.28
  182.2 5.2 copy-start.29
  187.5 142.6 %copy-start.24 = (f32[1024,16]{0,1:T(8,128)S(1)}, f32[1024,16]{0,1:T(8,128)}, u32[]{:S(2)}) copy-start(f32[1024,16]{0,1:T(8,128)} %broadcast_in_dim.318) | copy-start | bytes 196612
  187.5 142.6 %copy-start.25 = (f32[1024,16]{0,1:T(8,128)S(1)}, f32[1024,16]{0,1:T(8,128)}, u32[]{:S(2)}) copy-start(f32[1024,16]{0,1:T(8,128)} %broadcast_in_dim.325) | copy-start | bytes 196612
  187.5 142.6 %copy-start.27 = (pred[1024,16]{0,1:T(8,128)(4,1)S(1)}, pred[1024,16]{0,1:T(8,128)(4,1)}, u32[]{:S(2)}) copy-start(pred[1024,16]{0,1:T(8,128)(4,1)} %copy-done.26) | copy-start | bytes 49156
  189.3 1.9 copy-start.2
  198.2 1.9 copy-start.2
  216.1 1.9 copy-start.2
  225.0 1.9 copy-start.2
  233.9 1.9 copy-start.2
  242.8 1.9 copy-start.2
  251.7 1.9 copy-start.2
  260.6 1.9 copy-start.2
  269.6 1.9 copy-start.2
  278.5 1.9 copy-start.2
  332.5 7.9 copy-start.19
  332.5 7.9 copy-start.34
  340.4 13.4 %copy-start.3 = (bf16[1024,16,48]{2,1,0:T(8,128)(2,1)S(1)}, bf16[1024,16,48]{2,1,0:T(8,128)(2,1)}, u32[]{:S(2)}) copy-start(bf16[1024,16,48]{2,1,0:T(8,128)(2,1)} %copy.100) | copy-start | bytes 4718596
  353.8 2.8 copy-start.23
  353.8 3.0 copy-start.21
  353.8 3.1 copy-start.32
  357.2 100.8 %copy-start.5 = (bf16[1024,768]{0,1:T(8,128)(2,1)S(1)}, bf16[1024,768]{0,1:T(8,128)(2,1)}, u32[]{:S(2)}) copy-start(bf16[1024,768]{0,1:T(8,128)(2,1)} %copy-done.4) | copy-start | bytes 4718596
  458.0 228.4 %reduce-scatter.9.cloned.1.call-start = ((), (), s32[]{:S(2)}) async-start(), calls=%async_computation.5 | async-start | bytes 983040
  463.7 459.1 %all-reduce.3.cloned.1.call-start = ((), (), s32[]{:S(2)}) async-start(), calls=%async_computation.6 | async-start | bytes 18874368 | tf_op jit(solution)/shard_map/psum | solution.py:213
  675.3 5.5 copy-start.14
  703.0 5.5 copy-start.16
  731.2 5.0 copy-start.17
  731.2 5.0 copy-start.37
  736.2 2.5 copy-start.38
  922.7 3.4 copy-start.12
  926.1 2.5 copy-start.11
  928.6 2.5 copy-start.10
  928.6 3.9 copy-start.1
  (10 other events, 16.1 us)
Sparse Core Ops, SparseCore 0:
  458.1 26.4 reduce-scatter.6
  488.0 26.1 reduce-scatter.8
  731.3 191.3 all-reduce.2
where the time goes:
time: 954 us; the launch traced here: 939 us
  matrix products  421 us (44%)
  local copies, waits for them, and re-layouts  215 us (23%)
  waiting for transfers between devices  180 us (19%)
  other arithmetic  71.3 us (7%)
  blocking collectives  29.2 us (3%)
  between operations  15.2 us (2%)
    dot_general x224, matrix products, product(): jnp.einsum(pattern, left_side, right_side, preferred_element_type=jnp.flo...  380 us
    psum x1, waiting for transfers between devices, per_device(): lax.psum((grad_query, grad_key, grad_value, grad_outproj), ('seq', 'rep'))  180 us
    while x9, local copies, waits for them, and re-layouts, heads_map(): lax.map(lambda members: function(*members, pieces, scaling), transposed)  34.5 us
    while x32, local copies, waits for them, and re-layouts  30.9 us
    convert_element_type x6, local copies, waits for them, and re-layouts, sparse_rows(): dense.astype(jnp.float32)  30.7 us
    dot_general x8, matrix products, project(): return jnp.dot(left_side, right_side, preferred_element_type=jnp.float32)  24 us
  transfers between devices with their start and end apart: 4, of which 1 were waited for; matrix products, arithmetic and copies ran while one was open for 27% of the time, Pallas kernels for 0%

commit v1 on v0

--- a/solution.py
+++ b/solution.py
@@ -210,7 +210,7 @@
     grad_query = jnp.einsum("td,te->de", embedded, query_grad, preferred_element_type=jnp.float32)
     grad_key = jnp.einsum("td,te->de", embedded, key_grad, preferred_element_type=jnp.float32)
     grad_value = jnp.einsum("td,te->de", embedded, value_grad, preferred_element_type=jnp.float32)
-    summed = lax.psum((grad_query, grad_key, grad_value, grad_outproj), ("seq", "rep"))
+    summed = lax.psum(lax.psum((grad_query, grad_key, grad_value, grad_outproj), "seq"), "rep")
     return (encoded[None], embed_grad[None], summed[0], summed[1], summed[2], summed[3])
 
 

time: 954 us -> 1150 us (1.21)
  waiting for transfers between devices: 180 us -> 376 us
    psum x1 -> x2, waiting for transfers between devices: 180 us -> 376 us  [the longest x1 189 us: per_device(): lax.psum((grad_query, grad_key, grad_value, grad_outproj), 'seq')]
  transfers between devices with their start and end apart: 4 -> 5, of which waited for: 1 -> 2; matrix products, arithmetic and copies ran while one was open for 27% -> 23% of each run, Pallas kernels for 0% -> 0%
where the time goes in v1:
time: 1150 us; the launch traced here: 1130 us
  matrix products  421 us (37%)
  waiting for transfers between devices  376 us (33%)
  local copies, waits for them, and re-layouts  215 us (19%)
  other arithmetic  71.3 us (6%)
  blocking collectives  29.2 us (3%)
  between operations  15.2 us (1%)
    dot_general x224, matrix products, product(): jnp.einsum(pattern, left_side, right_side, preferred_element_type=jnp.flo...  380 us
    psum x1, waiting for transfers between devices, per_device(): lax.psum((grad_query, grad_key, grad_value, grad_outproj), 'seq')  189 us
    psum x1, waiting for transfers between devices, per_device(): lax.psum(lax.psum((grad_query, grad_key, grad_value, grad_outproj), 'seq'...  187 us
    while x9, local copies, waits for them, and re-layouts, heads_map(): lax.map(lambda members: function(*members, pieces, scaling), transposed)  34.5 us
    while x32, local copies, waits for them, and re-layouts  31 us
    convert_element_type x6, local copies, waits for them, and re-layouts, sparse_rows(): dense.astype(jnp.float32)  30.7 us
    dot_general x8, matrix products, project(): return jnp.dot(left_side, right_side, preferred_element_type=jnp.float32)  24 us
  transfers between devices with their start and end apart: 5, of which 2 were waited for; matrix products, arithmetic and copies ran while one was open for 23% of the time, Pallas kernels for 0%

profile of v1, /device:TPU:0, one launch (start us, length us, event | category | flops | bytes accessed | tf_op | source)
XLA Modules:
  0.0 1134.9 jit_solution(1358193090605964865)
XLA Ops:
  8.0 4.4 sort.17
  12.4 4.5 gather_fusion
  16.9 9.7 all_to_all.14
  26.6 4.0 gather_fusion.1
  32.0 4.5 all-to-all-start.1
  43.4 7.8 reshape.434
  53.2 4.9 copy.100
  58.1 6.4 scatter_custom_fusion
  69.9 7.8 reshape.431
  83.0 7.8 reshape.432
  90.9 4.3 convolution_convert_fusion
  98.2 7.8 reshape.433
  106.0 14.5 %select_reduce_fusion = (bf16[64,16,48]{2,1,0:T(8,128)(2,1)}, bf16[64,16,48]{2,1,0:T(8,128)(2,1)S(1)}, bf16[64,16,48]{2,1,0:T(8,128)(2,1)S(1)}, bf16[64,16,48]{2,1,0:T(8,128)(2,1)}) fusion(f32[64,16,16,48]{3,2,1,0:T(8,128)} %reshape.434, pred[16,16]{1,0:T(8,128)(4,1)S(1)} %iota_compare_fusion, f32[64,16,16,48]{3,2,1,0:T(8,128)} %reshape.432, ...), kind=kLoop, calls=%fused_computation.133 | loop fusion | flops 6094848 | bytes 12976384 | tf_op jit(solution)/shard_map/reduce_sum | solution.py:22
  120.7 10.6 all_gather.6
  132.3 8.9 all_gather.7
  143.8 26.0 %while.57 = (s32[]{:T(128)}, f32[16,64,48]{1,2,0:T(8,128)S(1)}, f32[16,64]{1,0:T(8,128)S(1)}, f32[16,64]{1,0:T(8,128)S(1)}, pred[16,256]{1,0:T(8,128)(4,1)S(1)},...) while((s32[]{:T(128)}, f32[16,64,48]{1,2,0:T(8,128)S(1)}, ...), condition=%wide.region_12.13_spmd, body=%wide.region_9.12_spmd.sunk | while | flops 3260290 | bytes 374129 | solution.py:86
  187.6 142.7 %while.56 = (s32[]{:T(128)}, f32[16,1024,48]{1,2,0:T(8,128)}, f32[16,1024]{1,0:T(8,128)S(1)}, f32[16,1024]{1,0:T(8,128)S(1)}, pred[16,1024]{1,0:T(8,128)(4,1)S(1...) while((s32[]{:T(128)}, f32[16,1024,48]{1,2,0:T(8,128)}, ...), condition=%wide.region_5.6_spmd, body=%wide.region_2.5_spmd.sunk | while | flops 212858880 | bytes 30383244 | solution.py:86
  201.4 4.0 fusion.202
  210.3 4.0 fusion.202
  219.2 4.0 fusion.202
  237.1 4.0 fusion.202
  246.0 4.0 fusion.202
  254.9 4.0 fusion.202
  263.8 4.0 fusion.202
  272.7 4.0 fusion.202
  299.5 4.0 fusion.202
  308.4 4.0 fusion.202
  317.3 4.0 fusion.202
  326.2 4.0 fusion.202
  332.8 7.9 copy.83
  340.7 13.4 %multiply_convert_fusion.1 = (bf16[1024,16,48]{2,1,0:T(8,128)(2,1)}, f32[1024,16,48]{2,1,0:T(8,128)S(1)}) fusion(f32[1024]{0:T(1024)S(1)} %copy-done.34, f32[1024,16]{1,0:T(8,128)} %copy.97, f32[1024,16]{1,0:T(8,128)S(1)} %copy.96, f32[64,16,48]{2,1,0:T(8,128)S(1)} %copy.95, pred[1024,16]{1,0:T(8,128)(4,1)S(1)} %copy-done.19, f32[1024,16]{1,0:T(8,128)S(1)} %copy.93, ...), kind=kLoop, calls=%fused_computation.135 | loop fusion | flops 5505024 | bytes 8278016 | tf_op jit(solution)/shard_map/convert_element_type | solution.py:154
  357.5 98.4 %while.59 = (s32[]{:T(128)}, f32[16,64,48]{1,2,0:T(8,128)S(1)}, f32[16,256,48]{1,2,0:T(8,128)}, f32[16,256,48]{1,2,0:T(8,128)}, pred[16,256]{1,0:T(8,128)(4,1)},...) while((s32[]{:T(128)}, f32[16,64,48]{1,2,0:T(8,128)S(1)}, ...), condition=%wide.region_20.21_spmd, body=%wide.region_19.20_spmd.sunk | while | flops 7994370 | bytes 687741 | solution.py:86
  470.6 181.2 %while.58 = (s32[]{:T(128)}, f32[16,1024,48]{1,2,0:T(8,128)}, f32[16,1024,48]{1,2,0:T(8,128)}, f32[16,1024,48]{1,2,0:T(8,128)}, pred[16,1024]{1,0:T(8,128)(4,1)S...) while((s32[]{:T(128)}, f32[16,1024,48]{1,2,0:T(8,128)}, ...), condition=%wide.region_15.16_spmd, body=%wide.region_14.15_spmd.sunk | while | flops 513900544 | bytes 21337212 | solution.py:86
  652.1 7.9 copy.102
  660.0 7.8 copy.112
  667.8 7.9 copy.115
  675.7 5.5 copy.98
  681.2 4.2 fusion.114
  688.2 15.2 %fusion.110 = (bf16[1024,16,48]{2,1,0:T(8,128)(2,1)}, bf16[1024,16,48]{2,1,0:T(8,128)(2,1)}, bf16[1024,16,48]{2,1,0:T(8,128)(2,1)}) fusion(f32[16,1024,48]{2,0,1:T(8,128)} %copy.102, f32[64,16,48]{2,1,0:T(8,128)S(1)} %copy.110, pred[1024,16]{1,0:T(8,128)(4,1)} %copy.94, f32[64,16,48]{2,1,0:T(8,128)S(1)} %copy.113, f32[16,1024,48]{2,0,1:T(8,128)} %copy.112, ...), kind=kLoop, calls=%fused_computation.127 | loop fusion | flops 7077888 | bytes 14761984 | tf_op jit(solution)/shard_map/convert_element_type | solution.py:194
  703.4 5.5 copy.111
  708.8 4.2 fusion.130
  713.1 5.5 copy.114
  718.6 4.2 fusion.131
  722.8 4.4 copy.117
  727.3 4.2 fusion.132
  731.6 188.9 %all-reduce.7.cloned.1.call-done = (f32[768,768]{1,0:T(8,128)}, f32[768,768]{1,0:T(8,128)}, f32[768,768]{1,0:T(8,128)}, f32[768,768]{1,0:T(8,128)}) async-done(((f32[768,768]{1,0:T(8,128)}, f32[768,768]{1,0:T(8,128)}, f32[768,768]{1,0:T(8,128)}, f32[768,768]{1,0:T(8,128)}), (f32[768,768]{1,0:T(8,128)}, f32[768,768]{1,0:T(8,128)}, f32[768,768]{1,0:T(8,128)}, ...) | async-done | bytes 9437200 | tf_op jit(solution)/shard_map/psum | solution.py:213
  920.5 5.0 fusion.117
  931.4 186.9 %all-reduce.5.cloned.1.call-done = (f32[768,768]{1,0:T(8,128)}, f32[768,768]{1,0:T(8,128)}, f32[768,768]{1,0:T(8,128)}, f32[768,768]{1,0:T(8,128)}) async-done(((f32[768,768]{1,0:T(8,128)}, f32[768,768]{1,0:T(8,128)}, f32[768,768]{1,0:T(8,128)}, f32[768,768]{1,0:T(8,128)}), (f32[768,768]{1,0:T(8,128)}, f32[768,768]{1,0:T(8,128)}, f32[768,768]{1,0:T(8,128)}, ...) | async-done | bytes 9437200 | tf_op jit(solution)/shard_map/psum | solution.py:213
  (599 shorter events, 482.6 us)
Async XLA Ops:
  7.2 19.4 %copy-start = (bf16[1,1024,768]{2,1,0:T(8,128)(2,1)S(1)}, bf16[1,1024,768]{2,1,0:T(8,128)(2,1)}, u32[]{:S(2)}) copy-start(bf16[1,1024,768]{2,1,0:T(8,128)(2,1)} %param.16) | copy-start | bytes 4718596
  32.0 6.4 copy-start.13
  32.0 26.1 %all-to-all-start.1 = ((bf16[4,256,768]{2,1,0:T(8,128)(2,1)}), bf16[4,256,768]{2,1,0:T(8,128)(2,1)}, u32[]{:S(2)}, u32[]{:S(2)}) async-start(bf16[4,256,768]{2,1,0:T(8,128)(2,1)} %broadcast_select_fusion), calls=%async_computation.1 | async-start | bytes 3145728 | tf_op jit(solution)/shard_map/all_to_all | solution.py:121
  36.5 648.9 %reduce-scatter.7.cloned.1.call-start = ((), (), s32[]{:S(2)}) async-start(), calls=%async_computation.4 | async-start | bytes 983040
  41.1 12.0 %copy-start.4 = (bf16[1024,768]{0,1:T(8,128)(2,1)}, bf16[1024,768]{0,1:T(8,128)(2,1)S(1)}, u32[]{:S(2)}) copy-start(bf16[1024,768]{0,1:T(8,128)(2,1)S(1)} %multiply_convert_fusion.2) | copy-start | bytes 4718596
  52.3 5.8 copy-start.26
  64.5 3.3 copy-start.15
  80.8 10.0 copy-start.6
  131.4 12.4 %copy-start.35 = (f32[16,64]{1,0:T(8,128)S(1)}, f32[16,64]{1,0:T(8,128)}, u32[]{:S(2)}) copy-start(f32[16,64]{1,0:T(8,128)} %custom-call.7) | copy-start | bytes 12292
  169.8 3.2 copy-start.9
  169.8 3.1 copy-start.22
  169.8 9.4 copy-start.30
  173.9 5.2 copy-start.7
  179.2 3.2 copy-start.8
  182.4 3.2 copy-start.36
  182.4 5.3 copy-start.28
  182.4 5.3 copy-start.29
  187.6 142.7 %copy-start.24 = (f32[1024,16]{0,1:T(8,128)S(1)}, f32[1024,16]{0,1:T(8,128)}, u32[]{:S(2)}) copy-start(f32[1024,16]{0,1:T(8,128)} %broadcast_in_dim.318) | copy-start | bytes 196612
  187.6 142.7 %copy-start.25 = (f32[1024,16]{0,1:T(8,128)S(1)}, f32[1024,16]{0,1:T(8,128)}, u32[]{:S(2)}) copy-start(f32[1024,16]{0,1:T(8,128)} %broadcast_in_dim.325) | copy-start | bytes 196612
  187.6 142.7 %copy-start.27 = (pred[1024,16]{0,1:T(8,128)(4,1)S(1)}, pred[1024,16]{0,1:T(8,128)(4,1)}, u32[]{:S(2)}) copy-start(pred[1024,16]{0,1:T(8,128)(4,1)} %copy-done.26) | copy-start | bytes 49156
  189.5 1.9 copy-start.2
  198.4 1.9 copy-start.2
  207.3 1.9 copy-start.2
  216.2 1.9 copy-start.2
  225.2 1.9 copy-start.2
  234.1 1.9 copy-start.2
  251.9 1.9 copy-start.2
  260.8 1.9 copy-start.2
  269.7 1.9 copy-start.2
  278.7 1.9 copy-start.2
  332.7 7.9 copy-start.19
  332.7 7.9 copy-start.34
  340.7 13.4 %copy-start.3 = (bf16[1024,16,48]{2,1,0:T(8,128)(2,1)S(1)}, bf16[1024,16,48]{2,1,0:T(8,128)(2,1)}, u32[]{:S(2)}) copy-start(bf16[1024,16,48]{2,1,0:T(8,128)(2,1)} %copy.100) | copy-start | bytes 4718596
  354.1 2.8 copy-start.23
  354.1 3.0 copy-start.21
  354.1 3.1 copy-start.32
  357.5 100.8 %copy-start.5 = (bf16[1024,768]{0,1:T(8,128)(2,1)S(1)}, bf16[1024,768]{0,1:T(8,128)(2,1)}, u32[]{:S(2)}) copy-start(bf16[1024,768]{0,1:T(8,128)(2,1)} %copy-done.4) | copy-start | bytes 4718596
  458.2 228.5 %reduce-scatter.9.cloned.1.call-start = ((), (), s32[]{:S(2)}) async-start(), calls=%async_computation.5 | async-start | bytes 983040
  463.9 456.6 %all-reduce.7.cloned.1.call-start = ((), (), s32[]{:S(2)}) async-start(), calls=%async_computation.7 | async-start | bytes 18874368 | tf_op jit(solution)/shard_map/psum | solution.py:213
  675.7 5.5 copy-start.14
  703.3 5.5 copy-start.16
  731.6 386.8 %all-reduce.5.cloned.1.call-start = ((), (), s32[]{:S(2)}) async-start(), calls=%async_computation.6 | async-start | bytes 18874368 | tf_op jit(solution)/shard_map/psum | solution.py:213
  920.5 5.0 copy-start.17
  920.5 5.0 copy-start.37
  1118.4 3.4 copy-start.12
  1121.7 2.5 copy-start.11
  1124.2 2.5 copy-start.10
  1124.2 3.9 copy-start.1
  (11 other events, 17.6 us)
Sparse Core Ops, SparseCore 0:
  458.4 26.4 reduce-scatter.6
  488.3 26.1 reduce-scatter.8
  731.7 188.7 all-reduce.6
  923.0 195.3 all-reduce.4
